TPU v7x, 32 devices: a whole 2x2x4 slice. The times are simulated.
32 devices in a mesh: row: 8 (over z, x), col: 4 (over y, core).
Axes of the slice: x: 2, y: 2, z: 4, core: 2. Of those that a mesh axis runs over, the one named last changes fastest.
Arguments:
- gradient: bfloat16 [3072, 14336], P('row', 'col'), may hold values from -0.1875 to 0.1875
- left_factor: float32 [3072, 3072], P('row', 'col'), may hold values from -1 to 11, as said below
- right_factor: float32 [14336, 14336], P('col', 'row'), may hold values from -1 to 3, as said below
- left_basis: bfloat16 [3072, 3072], P('row', 'col'), may hold values from -0.109375 to 0.109375
- right_basis: bfloat16 [14336, 2048], P('row', 'col'), may hold values from -0.046875 to 0.046875
Outputs:
- left_new: float32 [3072, 3072], P('row', 'col')
- right_new: float32 [14336, 14336], P('col', 'row')
- left_out: float32 [3072, 3072], P('row', 'col')
- right_out: float32 [14336, 2048], P('col', 'row')
Inputs may be any that keep to these rules, and one draw needn't show every extreme that they name: left_factor is symmetric. right_factor is symmetric.
All inputs are finite; a program needn't handle non-finite values.
Results may differ from a plain program's by a relative error of at most 0.0029.
Values may be sent and summed in bfloat16 or wider, within the bound.
A program may use at most 192 MiB of HBM per device.

v0:
```python
import functools

import jax
import jax.numpy as jnp
from jax import lax
from jax.experimental import pallas as pl
from jax.experimental.pallas import tpu as pltpu
from jax.sharding import PartitionSpec as P

ema_decay = 0.95
epsilon = 1e-06
MESH = pl.DeviceIdType.MESH
SLOTS = 4


def dot(a, b, dims):
    return lax.dot_general(a, b, (dims, ((), ())), preferred_element_type=jnp.float32)


def place_of(row, row_count):
    half = lax.div(row, 2)
    return jnp.where(lax.rem(row, 2) == 0, half, row_count - 1 - half)


def member_at(place, row_count):
    return jnp.where(place < row_count // 2, 2 * place, 2 * (row_count - 1 - place) + 1)


def greet(peers):
    barrier = pltpu.get_barrier_semaphore()
    for peer in peers:
        pl.semaphore_signal(barrier, inc=1, device_id=peer, device_id_type=MESH)
    pl.semaphore_wait(barrier, len(peers))


def gather_kernel(
    R, C, tile,
    grad, lb, rb, rf,
    right_out, left_out, lb_out, rb_out, match,
    acc, slab, own, rhs, left,
    load_sem, rf_sem, ring_send, ring_recv, match_send, match_recv, rhs_sem,
    lb_send, lb_recv, rb_send, rb_recv, keep_sem, out_sem,
):
    row, col = lax.axis_index("row"), lax.axis_index("col")
    rows, cols = grad.shape
    half = rows // 2
    ratio = R // C
    part = cols // ratio
    here = place_of(row, R)
    nxt = member_at(lax.rem(here + 1, R), R)
    prv = member_at(lax.rem(here + R - 1, R), R)
    toward = (nxt, prv)
    owner = lax.div(row, ratio)
    chosen = lax.rem(row, ratio)
    offset = lax.rem(col + C - owner, C)
    is_owner = offset == 0
    is_relay = jnp.logical_and(offset != 0, lax.rem(offset, 2) == 0)
    partner = col + 1 - 2 * lax.rem(col, 2)

    def origin(direction, t):
        there = here + R - t if direction == 0 else here + t
        return member_at(lax.rem(there, R), R)

    loads = []
    for s in range(ratio):
        lanes = pl.ds(s * part, part)
        for d in range(2):
            loads.append(pltpu.make_async_copy(
                grad.at[pl.ds(d * half, half), lanes], slab.at[0, d, s], load_sem.at[d, s]))
        loads.append(pltpu.make_async_copy(grad.at[:, lanes], own.at[s], load_sem.at[2, s]))
    for load in loads:
        load.start()
    load_rf = pltpu.make_async_copy(rf, acc, rf_sem)
    load_rf.start()
    keep_lb = pltpu.make_async_copy(
        lb, lb_out.at[pl.ds(pl.multiple_of(row * rows, 32), rows)], keep_sem.at[0])
    keep_rb = pltpu.make_async_copy(rb, rb_out.at[col], keep_sem.at[1])

    greet([{"row": nxt}, {"row": prv}] + [{"col": lax.rem(col + j, C)} for j in range(1, C)])

    def ring(t, d, s):
        return pltpu.make_async_remote_copy(
            src_ref=slab.at[t % SLOTS, d, s],
            dst_ref=slab.at[(t + 1) % SLOTS, d, s],
            send_sem=ring_send.at[t % 2, d, s],
            recv_sem=ring_recv.at[(t + 1) % SLOTS, d, s],
            device_id={"row": toward[d]}, device_id_type=MESH)

    def match_copy(t, d, j, source):
        target = partner if j == 0 else lax.rem(col + 2 * j, C)
        return pltpu.make_async_remote_copy(
            src_ref=source, dst_ref=match.at[t, d],
            send_sem=match_send.at[t % 2, d, j], recv_sem=match_recv.at[t, d],
            device_id={"col": target}, device_id_type=MESH)

    def offers(t):
        return [match_copy(t, d, j, slab.at[t % SLOTS, d, chosen])
                for d in range(2) for j in list(range(1, C // 2)) + [0]]

    def relays(t):
        return [match_copy(t, d, 0, match.at[t, d]) for d in range(2)]

    def offer(t):
        @pl.when(is_owner)
        def _():
            for copy in offers(t):
                copy.start()

    def settle(t):
        @pl.when(is_owner)
        def _():
            for copy in offers(t):
                copy.wait_send()

        @pl.when(is_relay)
        def _():
            for copy in relays(t):
                copy.wait_send()

    def relay(t):
        @pl.when(is_relay)
        def _():
            for copy in relays(t):
                copy.wait_recv()
                copy.start()

    def bring(t):
        @pl.when(is_owner)
        def _():
            for d in range(2):
                rhs[t % 2, d] = slab[t % SLOTS, d, chosen]

        @pl.when(jnp.logical_not(is_owner))
        def _():
            @pl.when(jnp.logical_not(is_relay))
            def _():
                for copy in relays(t):
                    copy.wait_recv()

            copies = [pltpu.make_async_copy(match.at[t, d], rhs.at[t % 2, d], rhs_sem.at[d])
                      for d in range(2)]
            for copy in copies:
                copy.start()
            for copy in copies:
                copy.wait()

    def write(row0):
        return pltpu.make_async_copy(
            acc.at[pl.ds(row0, tile)], right_out.at[pl.ds(row0, tile)], out_sem)

    def gram(t, s):
        @pl.loop(0, part // tile)
        def _(j):
            first = pl.multiple_of(j * tile, tile)
            block = jnp.concatenate(
                [slab[t % SLOTS, d, s, :, pl.ds(first, tile)] for d in range(2)], axis=0).T
            row0 = pl.multiple_of(s * part + j * tile, tile)
            for n in range(part // tile):
                lanes = slice(n * tile, (n + 1) * tile)
                other = rhs[t % 2, :, :, lanes].reshape(rows, tile)
                acc[pl.ds(row0, tile), lanes] += (1.0 - ema_decay) * dot(block, other, ((1,), (0,)))
            if t == R - 1:
                write(row0).start()

    def gram_left(t):
        for d in range(2):
            total = None
            for s in range(ratio):
                term = dot(slab[t % SLOTS, d, s], own[s], ((1,), (1,)))
                total = term if total is None else total + term
            row0 = pl.multiple_of(origin(d, t) * rows + d * half, 32)
            left[pl.ds(row0, half), :] = total

    def basis_ring(j, d):
        at = pl.ds(pl.multiple_of(origin(d, j) * rows + d * half, 32), half)
        return pltpu.make_async_remote_copy(
            src_ref=lb.at[pl.ds(d * half, half)] if j == 0 else lb_out.at[at],
            dst_ref=lb_out.at[at],
            send_sem=lb_send.at[j % 2, d], recv_sem=lb_recv.at[j, d],
            device_id={"row": toward[d]}, device_id_type=MESH)

    def basis_hop(j):
        for d in range(2):
            if j > 0:
                basis_ring(j - 1, d).wait_recv()
            if j < R - 1:
                if j > 1:
                    basis_ring(j - 2, d).wait_send()
                basis_ring(j, d).start()

    def vectors(j):
        target = partner if j == 0 else lax.rem(col + 2 * j, C)
        return pltpu.make_async_remote_copy(
            src_ref=rb, dst_ref=rb_out.at[col], send_sem=rb_send.at[0, j], recv_sem=rb_recv.at[col],
            device_id={"col": target}, device_id_type=MESH)

    def vectors_on(j):
        source = lax.rem(col + 2 * j, C)
        return pltpu.make_async_remote_copy(
            src_ref=rb_out.at[source], dst_ref=rb_out.at[source],
            send_sem=rb_send.at[1, j], recv_sem=rb_recv.at[source],
            device_id={"col": partner}, device_id_type=MESH)

    def vectors_in(source):
        return pltpu.make_async_remote_copy(
            src_ref=rb, dst_ref=rb_out.at[source], send_sem=rb_send.at[0, 0], recv_sem=rb_recv.at[source],
            device_id={"col": partner}, device_id_type=MESH)

    for load in loads:
        load.wait()
    for s in range(ratio):
        for d in range(2):
            ring(0, d, s).start()
    offer(0)
    keep_lb.start()
    keep_rb.start()
    for j in range(C // 2):
        vectors(j).start()
    load_rf.wait()

    @pl.loop(0, cols // tile)
    def _(j):
        at = pl.ds(pl.multiple_of(j * tile, tile), tile)
        acc[at, :] = acc[at, :] * ema_decay

    begin = R // 2
    for t in range(1, R):
        for s in range(ratio):
            for d in range(2):
                ring(t - 1, d, s).wait_recv()
            if t < R - 1:
                for d in range(2):
                    ring(t, d, s).start()

            if s == ratio - 1:
                offer(t)
                if t >= begin:
                    basis_hop(t - begin)
            if s == 0:
                relay(t - 1)
                bring(t - 1)
            gram(t - 1, s)
            if s == ratio - 1:
                gram_left(t - 1)
                settle(t - 1)
            for d in range(2):
                ring(t - 1, d, s).wait_send()
        if t == R // 2 - 1:
            for j in range(1, C // 2):
                vectors_in(lax.rem(col + 2 * j, C)).wait_recv()
                vectors_on(j).start()
    last = R - 1
    hops = list(range(R - begin, R))
    basis_hop(hops.pop(0))
    relay(last)
    if hops:
        basis_hop(hops.pop(0))
    bring(last)
    gram_left(last)
    put_left = pltpu.make_async_copy(left, left_out, keep_sem.at[2])
    put_left.start()
    for s in range(ratio):
        gram(last, s)
        if hops:
            basis_hop(hops.pop(0))
    settle(last)
    for hop in hops:
        basis_hop(hop)
    for d in range(2):
        for j in range(max(R - 3, 0), R - 1):
            basis_ring(j, d).wait_send()
    keep_lb.wait()
    keep_rb.wait()
    vectors_in(partner).wait_recv()
    for j in range(1, C // 2):
        vectors_in(lax.rem(partner + 2 * j, C)).wait_recv()
        vectors_on(j).wait_send()
    for j in range(C // 2):
        vectors(j).wait_send()
    put_left.wait()
    pltpu.make_async_copy(acc, right_out, out_sem).wait()


def gather_stage(R, C, gradient, left_basis, right_basis, right_factor):
    rows, cols = gradient.shape
    half, ratio = rows // 2, R // C
    part = cols // ratio
    tile = 256 if part % 256 == 0 else 128
    dmodel = rows * R
    any_space = pl.BlockSpec(memory_space=pl.ANY)
    dma = pltpu.SemaphoreType.DMA
    return pl.pallas_call(
        functools.partial(gather_kernel, R, C, tile),
        out_shape=(
            jax.ShapeDtypeStruct(right_factor.shape, jnp.float32),
            jax.ShapeDtypeStruct((dmodel, rows), jnp.float32),
            jax.ShapeDtypeStruct((dmodel, left_basis.shape[1]), jnp.bfloat16),
            jax.ShapeDtypeStruct((C,) + right_basis.shape, jnp.bfloat16),
            jax.ShapeDtypeStruct((R, 2, half, part), jnp.bfloat16),
        ),
        in_specs=[any_space] * 4,
        out_specs=(any_space,) * 5,
        scratch_shapes=[
            pltpu.VMEM(right_factor.shape, jnp.float32),
            pltpu.VMEM((SLOTS, 2, ratio, half, part), jnp.bfloat16),
            pltpu.VMEM((ratio, rows, part), jnp.bfloat16),
            pltpu.VMEM((2, 2, half, part), jnp.bfloat16),
            pltpu.VMEM((dmodel, rows), jnp.float32),
            dma((3, ratio)), dma, dma((2, 2, ratio)), dma((SLOTS, 2, ratio)),
            dma((2, 2, C // 2)), dma((R, 2)), dma((2,)),
            dma((2, 2)), dma((R - 1, 2)), dma((2, C // 2)), dma((C,)), dma((3,)), dma,
        ],
        compiler_params=pltpu.CompilerParams(
            collective_id=0, has_side_effects=True, vmem_limit_bytes=62 * 1024 * 1024),
        name="gather_gram",
    )(gradient, left_basis, right_basis, right_factor)


def product_kernel(
    R, C, m, dhidden,
    fresh, vectors, left_part, basis, left_factor,
    right_out, left_new_out, left_out,
    bv, xf, xh, rbuf, sbuf, prod, square, gather_sq,
    lparts, lhalf, lbasis, lfac, lnew, lprod, lsq,
    load_sem, x_sem, send_sem, recv_sem, sq_send, sq_recv,
    lp_send, lp_recv, lh_send, lh_recv, ls_send, ls_recv, out_sem,
):
    row, col = lax.axis_index("row"), lax.axis_index("col")
    total_rows, depth = fresh.shape
    lcols = left_factor.shape[1]
    dmodel = basis.shape[0]
    width = prod.shape[1]
    ratio = R // C
    H = R // 2
    count = total_rows // m
    hm = m // 2
    keep = xh.shape[0]
    here = place_of(row, R)
    toward = tuple(member_at(lax.rem(here + step, R), R) for step in (1, R - 1))

    load_v = pltpu.make_async_copy(vectors, bv, load_sem.at[0])
    load_b = pltpu.make_async_copy(basis, lbasis, load_sem.at[1])
    load_f = pltpu.make_async_copy(left_factor, lfac, load_sem.at[2])
    mine = pl.ds(pl.multiple_of(col * lcols, 128), lcols)
    load_p = pltpu.make_async_copy(left_part.at[mine], lparts.at[col], load_sem.at[3])
    load_v.start()

    def chunk(k):
        return pltpu.make_async_copy(
            fresh.at[pl.ds(pl.multiple_of(k * m, m), m)], xf.at[lax.rem(k, 2)], x_sem.at[lax.rem(k, 2)])

    chunk(0).start()
    load_b.start()
    load_f.start()
    load_p.start()
    greet([{"row": lax.rem(row + j, R)} for j in range(1, R)]
          + [{"col": lax.rem(col + j, C)} for j in range(1, C)])

    def other_col(j):
        return lax.rem(col + j, C)

    def part_copy(j):
        there = other_col(j)
        at = pl.ds(pl.multiple_of(there * lcols, 128), lcols)
        return pltpu.make_async_remote_copy(
            src_ref=left_part.at[at], dst_ref=lparts.at[col],
            send_sem=lp_send.at[j], recv_sem=lp_recv.at[col],
            device_id={"col": there}, device_id_type=MESH)

    def part_in(j):
        source = other_col(j)
        return pltpu.make_async_remote_copy(
            src_ref=left_part.at[mine], dst_ref=lparts.at[source],
            send_sem=lp_send.at[j], recv_sem=lp_recv.at[source],
            device_id={"col": source}, device_id_type=MESH)

    def half_copy(j, source):
        return pltpu.make_async_remote_copy(
            src_ref=lhalf.at[source], dst_ref=lhalf.at[source],
            send_sem=lh_send.at[j], recv_sem=lh_recv.at[source],
            device_id={"col": other_col(j)}, device_id_type=MESH)

    def lsq_copy(j, source):
        return pltpu.make_async_remote_copy(
            src_ref=lsq.at[source], dst_ref=lsq.at[source],
            send_sem=ls_send.at[j], recv_sem=ls_recv.at[source],
            device_id={"row": lax.rem(row + j, R)}, device_id_type=MESH)

    def sq_copy(j, source):
        return pltpu.make_async_remote_copy(
            src_ref=gather_sq.at[source], dst_ref=gather_sq.at[source],
            send_sem=sq_send.at[j], recv_sem=sq_recv.at[source],
            device_id={"col": other_col(j)}, device_id_type=MESH)

    new_out = pltpu.make_async_copy(lnew, left_new_out, out_sem.at[0])
    prod_out = pltpu.make_async_copy(lprod, left_out, out_sem.at[1])

    def left_sum():
        load_p.wait()
        load_f.wait()
        for j in range(1, C):
            part_in(j).wait_recv()
        total = lparts[0]
        for c in range(1, C):
            total = total + lparts[c]
        value = ema_decay * lfac[...] + (1.0 - ema_decay) * total.T
        lnew[...] = value
        lhalf[col] = value.astype(jnp.bfloat16)
        new_out.start()
        for j in range(1, C):
            half_copy(j, col).start()

    def left_product():
        load_b.wait()
        for j in range(1, C):
            half_copy(j, other_col(j)).wait_recv()
        total = None
        for c in range(C):
            term = dot(lhalf[c], lbasis[c * lcols:(c + 1) * lcols], ((1,), (0,)))
            total = term if total is None else total + term
        lprod[...] = total
        lsq[row] = jnp.broadcast_to(jnp.sum(total * total, axis=0, keepdims=True), lsq.shape[1:])
        for j in range(1, R):
            lsq_copy(j, row).start()

    def left_finish():
        for j in range(1, R):
            lsq_copy(j, lax.rem(row + j, R)).wait_recv()
        total = lsq[0]
        for r in range(1, R):
            total = total + lsq[r]
        lprod[...] = lprod[...] * lax.rsqrt(total[0:1] / dmodel + epsilon)
        prod_out.start()

    def message(t, d, h):
        rows = pl.ds(d * hm, hm) if h == 0 else pl.ds(0, m)
        return pltpu.make_async_remote_copy(
            src_ref=sbuf.at[lax.rem(t, 2), d, h, rows],
            dst_ref=rbuf.at[lax.rem(t, 4), d, h, rows],
            send_sem=send_sem.at[lax.rem(t, 2), d, h],
            recv_sem=recv_sem.at[lax.rem(t, 4), d, h],
            device_id={"row": toward[d]}, device_id_type=MESH)

    def block(k, dest, rows):
        source = lax.div(dest, ratio)
        lanes = pl.ds(pl.multiple_of(lax.rem(dest, ratio) * width, 128), width)
        return dot(xh[lax.rem(k, keep), rows], bv[source, :, lanes], ((1,), (0,)))

    def dest_of(d, h):
        away = H - h if d == 0 else R - (H - h)
        return member_at(lax.rem(here + away, R), R)

    def ready(k):
        return jnp.logical_and(k >= 0, k < count)

    for j in range(1, C):
        part_copy(j).start()
    square[...] = jnp.zeros_like(square)
    load_v.wait()
    steps = count + H

    @pl.loop(0, steps)
    def _(t):
        @pl.when(t < count)
        def _():
            chunk(t).wait()

            @pl.when(t + 1 < count)
            def _():
                chunk(t + 1).start()

            xh[lax.rem(t, keep)] = xf[lax.rem(t, 2)].astype(jnp.bfloat16)

        @pl.when(ready(t - H))
        def _():
            k = t - H
            total = block(k, row, slice(0, m))
            for d in range(2):
                message(t - 1, d, H - 1).wait_recv()
                total = total + rbuf[lax.rem(t - 1, 4), d, H - 1].astype(jnp.float32)
            prod[pl.ds(pl.multiple_of(k * m, m), m), :] = total
            square[...] += jnp.sum(total * total, axis=0, keepdims=True)

        for h in range(H - 1, -1, -1):
            @pl.when(ready(t - h))
            def _():
                k = t - h
                for d in range(2):
                    @pl.when(k >= 2)
                    def _():
                        message(t - 2, d, h).wait_send()

                    dest = dest_of(d, h)
                    slot = lax.rem(t, 2)
                    some = slice(d * hm, d * hm + hm)
                    rest = slice(hm - d * hm, m - d * hm)
                    if h == 0:
                        sbuf[slot, d, h, some] = block(k, dest, some).astype(jnp.bfloat16)
                    else:
                        fresh_part = block(k, dest, slice(0, m))
                        message(t - 1, d, h - 1).wait_recv()
                        if h == 1:
                            came = rbuf[lax.rem(t - 1, 4), d, 0, some].astype(jnp.float32)
                            sbuf[slot, d, h, some] = (fresh_part[some] + came).astype(jnp.bfloat16)
                            sbuf[slot, d, h, rest] = fresh_part[rest].astype(jnp.bfloat16)
                        else:
                            came = rbuf[lax.rem(t - 1, 4), d, h - 1].astype(jnp.float32)
                            sbuf[slot, d, h] = (fresh_part + came).astype(jnp.bfloat16)
                    message(t, d, h).start()

        for at, work in ((6, left_sum), (8, left_product), (10, left_finish)):
            pl.when(t == min(at, steps - 1))(work)

    gather_sq[col] = jnp.broadcast_to(square[...], gather_sq.shape[1:])
    for j in range(1, C):
        sq_copy(j, col).start()
    for d in range(2):
        for h in range(H):
            for k in (count - 2, count - 1):
                message(k + h, d, h).wait_send()
    for j in range(1, C):
        part_copy(j).wait_send()
        half_copy(j, col).wait_send()
    for j in range(1, R):
        lsq_copy(j, row).wait_send()
    new_out.wait()
    prod_out.wait()
    for j in range(1, C):
        sq_copy(j, other_col(j)).wait_recv()
    total = gather_sq[0]
    for c in range(1, C):
        total = total + gather_sq[c]
    scale = lax.rsqrt(total[0:1] / dhidden + epsilon)

    def put(k):
        at = pl.ds(pl.multiple_of(k * m, m), m)
        return pltpu.make_async_copy(prod.at[at], right_out.at[at], out_sem.at[2])

    @pl.loop(0, count)
    def _(k):
        at = pl.ds(pl.multiple_of(k * m, m), m)
        prod[at, :] = prod[at, :] * scale
        put(k).start()

    for j in range(1, C):
        sq_copy(j, col).wait_send()
    pltpu.make_async_copy(prod, right_out, out_sem.at[2]).wait()


def product_stage(R, C, dhidden, fresh, vectors, left_part, basis, left_factor):
    total_rows, depth = fresh.shape
    m = 256
    H = R // 2
    width = vectors.shape[0] * vectors.shape[2] // R
    rows, lcols = left_factor.shape
    any_space = pl.BlockSpec(memory_space=pl.ANY)
    dma = pltpu.SemaphoreType.DMA
    f32, bf16 = jnp.float32, jnp.bfloat16
    return pl.pallas_call(
        functools.partial(product_kernel, R, C, m, dhidden),
        out_shape=(
            jax.ShapeDtypeStruct((total_rows, width), f32),
            jax.ShapeDtypeStruct((rows, lcols), f32),
            jax.ShapeDtypeStruct((rows, lcols), f32),
        ),
        in_specs=[any_space] * 5,
        out_specs=(any_space,) * 3,
        scratch_shapes=[
            pltpu.VMEM(vectors.shape, bf16),
            pltpu.VMEM((2, m, depth), f32),
            pltpu.VMEM((H + 1, m, depth), bf16),
            pltpu.VMEM((4, 2, H, m, width), bf16),
            pltpu.VMEM((2, 2, H, m, width), bf16),
            pltpu.VMEM((total_rows, width), f32),
            pltpu.VMEM((1, width), f32),
            pltpu.VMEM((C, 8, width), f32),
            pltpu.VMEM((C, lcols, rows), f32),
            pltpu.VMEM((C, rows, lcols), bf16),
            pltpu.VMEM(basis.shape, bf16),
            pltpu.VMEM((rows, lcols), f32),
            pltpu.VMEM((rows, lcols), f32),
            pltpu.VMEM((rows, lcols), f32),
            pltpu.VMEM((R, 8, lcols), f32),
            dma((4,)), dma((2,)), dma((2, 2, H)), dma((4, 2, H)), dma((C,)), dma((C,)),
            dma((C,)), dma((C,)), dma((C,)), dma((C,)), dma((R,)), dma((R,)), dma((3,)),
        ],
        compiler_params=pltpu.CompilerParams(
            collective_id=1, has_side_effects=True, vmem_limit_bytes=62 * 1024 * 1024),
        name="product_reduce",
    )(fresh, vectors, left_part, basis, left_factor)


def make_body(R, C, dhidden):
    def on_device(gradient, left_factor, right_factor, left_basis, right_basis):
        right_new, gram_part, left_basis_cols, vectors, _ = gather_stage(
            R, C, gradient, left_basis, right_basis, right_factor)
        right_out, left_new, left_out = product_stage(
            R, C, dhidden, right_new, vectors, gram_part, left_basis_cols, left_factor)
        return (left_new, right_new, left_out, right_out)

    return on_device


def solution(mesh):
    in_specs = (P("row", "col"), P("row", "col"), P("col", "row"), P("row", "col"), P("row", "col"))
    out_specs = (P("row", "col"), P("col", "row"), P("row", "col"), P("col", "row"))

    def step(gradient, left_factor, right_factor, left_basis, right_basis):
        body = make_body(mesh.shape["row"], mesh.shape["col"], gradient.shape[1])
        return jax.shard_map(
            body, mesh=mesh, in_specs=in_specs, out_specs=out_specs, check_vma=False
        )(gradient, left_factor, right_factor, left_basis, right_basis)

    return step
```

profile of v0, /device:TPU:0, one launch (start us, length us, event | category | flops | bytes accessed | tf_op | source)
XLA Modules:
  0.0 453.9 jit_solution(5192731683071628939)
XLA Ops:
  0.6 271.3 %gather_gram.1 = (f32[3584,1792]{1,0:T(8,128)}, f32[3072,384]{1,0:T(8,128)}, bf16[3072,768]{1,0:T(8,128)(2,1)}, bf16[4,1792,512]{2,1,0:T(8,128)(2,1)}, bf16[8,2,192,1792]{3,2,1,0:T(8,128)(2,1)}) custom-call(bf16[384,3584]{1,0:T(8,128)(2,1)} %grad.1, bf16[384,768]{1,0:T(8,128)(2,1)} %lb.1, bf16[1792,512]{1,0:T(8,128)(2,1)} %rb.1, f32[3584,1792]{1,0:T(8,128)} %rf.1), custom_call_target="tpu_custom_call" | custom-call | tf_op jit(solution)/shard_map/gather_gram/pallas_call | solution.py:292
  271.9 158.0 %product_reduce.1 = (f32[3584,256]{1,0:T(8,128)}, f32[384,768]{1,0:T(8,128)}, f32[384,768]{1,0:T(8,128)}) custom-call(f32[3584,1792]{1,0:T(8,128)} %get-tuple-element.23.fresh, bf16[4,1792,512]{2,1,0:T(8,128)(2,1)} %get-tuple-element.12.vectors, f32[3072,384]{1,0:T(8,128)} %get-tuple-element.13.left_part, bf16[3072,768]{1,0:T(8,128)(2,1)} %get-tuple-element.14.basis, ...), custom_call_target="tpu_custom_call" | custom-call | tf_op jit(solution)/shard_map/product_reduce/pallas_call | solution.py:559
  429.9 2.4 copy.13
  432.3 0.0 copy-start.1
  432.3 0.0 copy-start
  432.3 18.7 %copy.14 = f32[3584,1792]{1,0:T(8,128)} copy(f32[3584,1792]{1,0:T(8,128)} %get-tuple-element.23.fresh) | data formatting | bytes 51380224
  451.0 0.0 copy-done.1
  451.0 1.0 copy.15
  452.0 0.0 copy-done
  452.1 1.8 copy.16
Async XLA Ops:
  432.3 18.8 %copy-start.1 = (f32[384,768]{1,0:T(8,128)S(1)}, f32[384,768]{1,0:T(8,128)}, u32[]{:S(2)}) copy-start(f32[384,768]{1,0:T(8,128)} %get-tuple-element.24) | copy-start | bytes 3538948
  432.3 19.8 %copy-start = (f32[3584,256]{1,0:T(8,128)S(1)}, f32[3584,256]{1,0:T(8,128)}, u32[]{:S(2)}) copy-start(f32[3584,256]{1,0:T(8,128)} %get-tuple-element.25) | copy-start | bytes 11010052
where the time goes:
time: 454 us
  Pallas kernels  429 us (94%)
  local copies, waits for them, and re-layouts  24 us (5%)
    pallas_call x1, Pallas kernels, gather_stage(): pl.pallas_call(functools.partial(gather_kernel, R, C, tile), out_shape=(j...  271 us
    pallas_call x1, Pallas kernels, product_stage(): pl.pallas_call(functools.partial(product_kernel, R, C, m, dhidden), out_s...  158 us
    unnamed x8, local copies, waits for them, and re-layouts  24 us

commit v1 on v0

--- a/solution.py
+++ b/solution.py
@@ -11,6 +11,8 @@
 epsilon = 1e-06
 MESH = pl.DeviceIdType.MESH
 SLOTS = 4
+SPLIT = 2
+CHUNK = 256
 
 
 def dot(a, b, dims):
@@ -36,7 +38,7 @@
 def gather_kernel(
     R, C, tile,
     grad, lb, rb, rf,
-    right_out, left_out, lb_out, rb_out, match,
+    partial_out, left_out, lb_out, rb_out, last_out, last_match, match,
     acc, slab, own, rhs, left,
     load_sem, rf_sem, ring_send, ring_recv, match_send, match_recv, rhs_sem,
     lb_send, lb_recv, rb_send, rb_recv, keep_sem, out_sem,
@@ -51,7 +53,9 @@
     prv = member_at(lax.rem(here + R - 1, R), R)
     toward = (nxt, prv)
     owner = lax.div(row, ratio)
-    chosen = lax.rem(row, ratio)
+    quarter = half // SPLIT
+    chosen = pl.ds(pl.multiple_of(lax.rem(row, ratio) * part, 128), part)
+    last = R - 1
     offset = lax.rem(col + C - owner, C)
     is_owner = offset == 0
     is_relay = jnp.logical_and(offset != 0, lax.rem(offset, 2) == 0)
@@ -61,14 +65,12 @@
         there = here + R - t if direction == 0 else here + t
         return member_at(lax.rem(there, R), R)
 
-    loads = []
-    for s in range(ratio):
-        lanes = pl.ds(s * part, part)
+    loads = [pltpu.make_async_copy(grad, own, load_sem.at[2, 0])]
+    for s in range(SPLIT):
         for d in range(2):
             loads.append(pltpu.make_async_copy(
-                grad.at[pl.ds(d * half, half), lanes], slab.at[0, d, s], load_sem.at[d, s]))
-        loads.append(pltpu.make_async_copy(grad.at[:, lanes], own.at[s], load_sem.at[2, s]))
-    for load in loads:
+                grad.at[pl.ds(d * half + s * quarter, quarter)], slab.at[0, d, s], load_sem.at[d, s]))
+    for load in reversed(loads):
         load.start()
     load_rf = pltpu.make_async_copy(rf, acc, rf_sem)
     load_rf.start()
@@ -86,96 +88,97 @@
             recv_sem=ring_recv.at[(t + 1) % SLOTS, d, s],
             device_id={"row": toward[d]}, device_id_type=MESH)
 
-    def match_copy(t, d, j, source):
+    def landed(t, d, s):
+        return last_match.at[d, s] if t == last else match.at[t, d, s]
+
+    def match_copy(t, d, s, j, source):
         target = partner if j == 0 else lax.rem(col + 2 * j, C)
         return pltpu.make_async_remote_copy(
-            src_ref=source, dst_ref=match.at[t, d],
-            send_sem=match_send.at[t % 2, d, j], recv_sem=match_recv.at[t, d],
+            src_ref=source, dst_ref=landed(t, d, s),
+            send_sem=match_send.at[t % 2, d, s, j], recv_sem=match_recv.at[t, d, s],
             device_id={"col": target}, device_id_type=MESH)
 
-    def offers(t):
-        return [match_copy(t, d, j, slab.at[t % SLOTS, d, chosen])
+    def offers(t, s):
+        return [match_copy(t, d, s, j, slab.at[t % SLOTS, d, s, :, chosen])
                 for d in range(2) for j in list(range(1, C // 2)) + [0]]
 
-    def relays(t):
-        return [match_copy(t, d, 0, match.at[t, d]) for d in range(2)]
-
-    def offer(t):
+    def relays(t, s):
+        return [match_copy(t, d, s, 0, landed(t, d, s)) for d in range(2)]
+
+    def offer(t, s):
         @pl.when(is_owner)
         def _():
-            for copy in offers(t):
+            for copy in offers(t, s):
                 copy.start()
 
     def settle(t):
-        @pl.when(is_owner)
-        def _():
-            for copy in offers(t):
-                copy.wait_send()
-
+        for s in range(SPLIT):
+            @pl.when(is_owner)
+            def _():
+                for copy in offers(t, s):
+                    copy.wait_send()
+
+            @pl.when(is_relay)
+            def _():
+                for copy in relays(t, s):
+                    copy.wait_send()
+
+    def relay(t, s):
         @pl.when(is_relay)
         def _():
-            for copy in relays(t):
-                copy.wait_send()
-
-    def relay(t):
-        @pl.when(is_relay)
-        def _():
-            for copy in relays(t):
+            for copy in relays(t, s):
                 copy.wait_recv()
                 copy.start()
 
+    def arrive(t):
+        @pl.when(jnp.logical_not(jnp.logical_or(is_owner, is_relay)))
+        def _():
+            for s in range(SPLIT):
+                for copy in relays(t, s):
+                    copy.wait_recv()
+
     def bring(t):
+        arrive(t)
+
         @pl.when(is_owner)
         def _():
             for d in range(2):
-                rhs[t % 2, d] = slab[t % SLOTS, d, chosen]
+                for s in range(SPLIT):
+                    rhs[t % 2, d, s] = slab[t % SLOTS, d, s, :, chosen]
 
         @pl.when(jnp.logical_not(is_owner))
         def _():
-            @pl.when(jnp.logical_not(is_relay))
-            def _():
-                for copy in relays(t):
-                    copy.wait_recv()
-
-            copies = [pltpu.make_async_copy(match.at[t, d], rhs.at[t % 2, d], rhs_sem.at[d])
-                      for d in range(2)]
-            for copy in copies:
-                copy.start()
-            for copy in copies:
-                copy.wait()
+            copy = pltpu.make_async_copy(match.at[t], rhs.at[t % 2], rhs_sem.at[0])
+            copy.start()
+            copy.wait()
 
     def write(row0):
         return pltpu.make_async_copy(
-            acc.at[pl.ds(row0, tile)], right_out.at[pl.ds(row0, tile)], out_sem)
+            acc.at[pl.ds(row0, tile)], partial_out.at[pl.ds(row0, tile)], out_sem)
 
     def gram(t, s):
         @pl.loop(0, part // tile)
         def _(j):
             first = pl.multiple_of(j * tile, tile)
-            block = jnp.concatenate(
-                [slab[t % SLOTS, d, s, :, pl.ds(first, tile)] for d in range(2)], axis=0).T
-            row0 = pl.multiple_of(s * part + j * tile, tile)
+            row0 = pl.multiple_of(s * part + first, tile)
+            block = slab[t % SLOTS, :, :, :, pl.ds(row0, tile)].reshape(rows, tile).T
             for n in range(part // tile):
                 lanes = slice(n * tile, (n + 1) * tile)
-                other = rhs[t % 2, :, :, lanes].reshape(rows, tile)
+                other = rhs[t % 2, :, :, :, lanes].reshape(rows, tile)
                 acc[pl.ds(row0, tile), lanes] += (1.0 - ema_decay) * dot(block, other, ((1,), (0,)))
-            if t == R - 1:
+            if t == last - 1:
                 write(row0).start()
 
     def gram_left(t):
         for d in range(2):
-            total = None
-            for s in range(ratio):
-                term = dot(slab[t % SLOTS, d, s], own[s], ((1,), (1,)))
-                total = term if total is None else total + term
+            total = dot(slab[t % SLOTS, d].reshape(half, cols), own[...], ((1,), (1,)))
             row0 = pl.multiple_of(origin(d, t) * rows + d * half, 32)
             left[pl.ds(row0, half), :] = total
 
     def basis_ring(j, d):
-        at = pl.ds(pl.multiple_of(origin(d, j) * rows + d * half, 32), half)
-        return pltpu.make_async_remote_copy(
-            src_ref=lb.at[pl.ds(d * half, half)] if j == 0 else lb_out.at[at],
-            dst_ref=lb_out.at[at],
+        at = pl.ds(pl.multiple_of(origin(d, j) * rows, 32), rows)
+        return pltpu.make_async_remote_copy(
+            src_ref=lb if j == 0 else lb_out.at[at], dst_ref=lb_out.at[at],
             send_sem=lb_send.at[j % 2, d], recv_sem=lb_recv.at[j, d],
             device_id={"row": toward[d]}, device_id_type=MESH)
 
@@ -183,7 +186,8 @@
         for d in range(2):
             if j > 0:
                 basis_ring(j - 1, d).wait_recv()
-            if j < R - 1:
+        for d in range(2):
+            if j < hops:
                 if j > 1:
                     basis_ring(j - 2, d).wait_send()
                 basis_ring(j, d).start()
@@ -206,12 +210,13 @@
             src_ref=rb, dst_ref=rb_out.at[source], send_sem=rb_send.at[0, 0], recv_sem=rb_recv.at[source],
             device_id={"col": partner}, device_id_type=MESH)
 
-    for load in loads:
+    for load in reversed(loads):
         load.wait()
-    for s in range(ratio):
+    for s in range(SPLIT):
         for d in range(2):
             ring(0, d, s).start()
-    offer(0)
+    for s in range(SPLIT):
+        offer(0, s)
     keep_lb.start()
     keep_rb.start()
     for j in range(C // 2):
@@ -223,24 +228,29 @@
         at = pl.ds(pl.multiple_of(j * tile, tile), tile)
         acc[at, :] = acc[at, :] * ema_decay
 
-    begin = R // 2
+    relay_due = [(0, s) for s in range(SPLIT)]
+    hops = R // 2 - 2
+    begin = R - hops
     for t in range(1, R):
-        for s in range(ratio):
+        for s in range(SPLIT):
             for d in range(2):
                 ring(t - 1, d, s).wait_recv()
-            if t < R - 1:
+            if t < last:
                 for d in range(2):
                     ring(t, d, s).start()
-
-            if s == ratio - 1:
-                offer(t)
-                if t >= begin:
-                    basis_hop(t - begin)
+            offer(t, s)
+            if s == SPLIT - 1 and t >= begin:
+                basis_hop(t - begin)
+            for due in relay_due:
+                relay(*due)
+            relay_due = [(t, s)]
             if s == 0:
-                relay(t - 1)
                 bring(t - 1)
-            gram(t - 1, s)
-            if s == ratio - 1:
+            if s < SPLIT - 1:
+                gram(t - 1, s)
+            else:
+                for rest in range(s, ratio):
+                    gram(t - 1, rest)
                 gram_left(t - 1)
                 settle(t - 1)
             for d in range(2):
@@ -249,26 +259,31 @@
             for j in range(1, C // 2):
                 vectors_in(lax.rem(col + 2 * j, C)).wait_recv()
                 vectors_on(j).start()
-    last = R - 1
-    hops = list(range(R - begin, R))
-    basis_hop(hops.pop(0))
-    relay(last)
-    if hops:
-        basis_hop(hops.pop(0))
-    bring(last)
+    put_last = pltpu.make_async_copy(slab.at[last % SLOTS], last_out, keep_sem.at[3])
+    put_last.start()
+    own_match = pltpu.make_async_copy(slab.at[last % SLOTS, :, :, :, chosen], last_match, rhs_sem.at[1])
+
+    @pl.when(is_owner)
+    def _():
+        own_match.start()
+
     gram_left(last)
     put_left = pltpu.make_async_copy(left, left_out, keep_sem.at[2])
     put_left.start()
-    for s in range(ratio):
-        gram(last, s)
-        if hops:
-            basis_hop(hops.pop(0))
+    for due in relay_due:
+        relay(*due)
+    arrive(last)
     settle(last)
-    for hop in hops:
-        basis_hop(hop)
+    basis_hop(hops)
     for d in range(2):
-        for j in range(max(R - 3, 0), R - 1):
+        for j in range(max(hops - 2, 0), hops):
             basis_ring(j, d).wait_send()
+
+    @pl.when(is_owner)
+    def _():
+        own_match.wait()
+
+    put_last.wait()
     keep_lb.wait()
     keep_rb.wait()
     vectors_in(partner).wait_recv()
@@ -278,13 +293,13 @@
     for j in range(C // 2):
         vectors(j).wait_send()
     put_left.wait()
-    pltpu.make_async_copy(acc, right_out, out_sem).wait()
+    pltpu.make_async_copy(acc, partial_out, out_sem).wait()
 
 
 def gather_stage(R, C, gradient, left_basis, right_basis, right_factor):
     rows, cols = gradient.shape
     half, ratio = rows // 2, R // C
-    part = cols // ratio
+    part, quarter = cols // ratio, half // SPLIT
     tile = 256 if part % 256 == 0 else 128
     dmodel = rows * R
     any_space = pl.BlockSpec(memory_space=pl.ANY)
@@ -296,19 +311,21 @@
             jax.ShapeDtypeStruct((dmodel, rows), jnp.float32),
             jax.ShapeDtypeStruct((dmodel, left_basis.shape[1]), jnp.bfloat16),
             jax.ShapeDtypeStruct((C,) + right_basis.shape, jnp.bfloat16),
-            jax.ShapeDtypeStruct((R, 2, half, part), jnp.bfloat16),
+            jax.ShapeDtypeStruct((2, SPLIT, quarter, cols), jnp.bfloat16),
+            jax.ShapeDtypeStruct((2, SPLIT, quarter, part), jnp.bfloat16),
+            jax.ShapeDtypeStruct((R - 1, 2, SPLIT, quarter, part), jnp.bfloat16),
         ),
         in_specs=[any_space] * 4,
-        out_specs=(any_space,) * 5,
+        out_specs=(any_space,) * 7,
         scratch_shapes=[
             pltpu.VMEM(right_factor.shape, jnp.float32),
-            pltpu.VMEM((SLOTS, 2, ratio, half, part), jnp.bfloat16),
-            pltpu.VMEM((ratio, rows, part), jnp.bfloat16),
-            pltpu.VMEM((2, 2, half, part), jnp.bfloat16),
+            pltpu.VMEM((SLOTS, 2, SPLIT, quarter, cols), jnp.bfloat16),
+            pltpu.VMEM((rows, cols), jnp.bfloat16),
+            pltpu.VMEM((2, 2, SPLIT, quarter, part), jnp.bfloat16),
             pltpu.VMEM((dmodel, rows), jnp.float32),
-            dma((3, ratio)), dma, dma((2, 2, ratio)), dma((SLOTS, 2, ratio)),
-            dma((2, 2, C // 2)), dma((R, 2)), dma((2,)),
-            dma((2, 2)), dma((R - 1, 2)), dma((2, C // 2)), dma((C,)), dma((3,)), dma,
+            dma((3, SPLIT)), dma, dma((2, 2, SPLIT)), dma((SLOTS, 2, SPLIT)),
+            dma((2, 2, SPLIT, C // 2)), dma((R, 2, SPLIT)), dma((2,)),
+            dma((2, 2)), dma((R - 1, 2)), dma((2, C // 2)), dma((C,)), dma((4,)), dma,
         ],
         compiler_params=pltpu.CompilerParams(
             collective_id=0, has_side_effects=True, vmem_limit_bytes=62 * 1024 * 1024),
@@ -318,16 +335,16 @@
 
 def product_kernel(
     R, C, m, dhidden,
-    fresh, vectors, left_part, basis, left_factor,
-    right_out, left_new_out, left_out,
-    bv, xf, xh, rbuf, sbuf, prod, square, gather_sq,
+    fresh, vectors, left_part, basis, came_forward, came_back, left_factor,
+    right_out, square_out, left_new_out, left_out,
+    bv, xf, xh, rbuf, sbuf, prod, square, gather_sq, sum_sq,
     lparts, lhalf, lbasis, lfac, lnew, lprod, lsq,
     load_sem, x_sem, send_sem, recv_sem, sq_send, sq_recv,
-    lp_send, lp_recv, lh_send, lh_recv, ls_send, ls_recv, out_sem,
+    lp_send, lp_recv, lh_send, lh_recv, ls_send, ls_recv, lb_send, lb_recv, out_sem,
 ):
     row, col = lax.axis_index("row"), lax.axis_index("col")
     total_rows, depth = fresh.shape
-    lcols = left_factor.shape[1]
+    rows, lcols = left_factor.shape
     dmodel = basis.shape[0]
     width = prod.shape[1]
     ratio = R // C
@@ -338,11 +355,19 @@
     here = place_of(row, R)
     toward = tuple(member_at(lax.rem(here + step, R), R) for step in (1, R - 1))
 
+    def origin_rows(d, j, side=None):
+        there = here + R - j if d == 0 else here + j
+        first = member_at(lax.rem(there, R), R) * rows
+        if side is None:
+            return pl.ds(pl.multiple_of(first, 32), rows)
+        return pl.ds(pl.multiple_of(first + side * (rows // 2), 32), rows // 2)
+
     load_v = pltpu.make_async_copy(vectors, bv, load_sem.at[0])
     load_b = pltpu.make_async_copy(basis, lbasis, load_sem.at[1])
     load_f = pltpu.make_async_copy(left_factor, lfac, load_sem.at[2])
     mine = pl.ds(pl.multiple_of(col * lcols, 128), lcols)
     load_p = pltpu.make_async_copy(left_part.at[mine], lparts.at[col], load_sem.at[3])
+    load_b.start()
     load_v.start()
 
     def chunk(k):
@@ -350,9 +375,15 @@
             fresh.at[pl.ds(pl.multiple_of(k * m, m), m)], xf.at[lax.rem(k, 2)], x_sem.at[lax.rem(k, 2)])
 
     chunk(0).start()
-    load_b.start()
     load_f.start()
     load_p.start()
+    load_b.wait()
+    pieces = [
+        pltpu.make_async_copy(piece, lbasis.at[origin_rows(d, H - 1)], load_sem.at[4 + d])
+        for d, piece in enumerate((came_forward, came_back))
+    ]
+    for piece in pieces:
+        piece.start()
     greet([{"row": lax.rem(row + j, R)} for j in range(1, R)]
           + [{"col": lax.rem(col + j, C)} for j in range(1, C)])
 
@@ -410,8 +441,16 @@
         for j in range(1, C):
             half_copy(j, col).start()
 
+    def basis_ring(d):
+        at = origin_rows(d, H - 1, d)
+        return pltpu.make_async_remote_copy(
+            src_ref=lbasis.at[at], dst_ref=lbasis.at[at],
+            send_sem=lb_send.at[d], recv_sem=lb_recv.at[d],
+            device_id={"row": toward[d]}, device_id_type=MESH)
+
     def left_product():
-        load_b.wait()
+        for d in range(2):
+            basis_ring(d).wait_recv()
         for j in range(1, C):
             half_copy(j, other_col(j)).wait_recv()
         total = None
@@ -453,6 +492,10 @@
     def ready(k):
         return jnp.logical_and(k >= 0, k < count)
 
+    for piece in pieces:
+        piece.wait()
+    for d in range(2):
+        basis_ring(d).start()
     for j in range(1, C):
         part_copy(j).start()
     square[...] = jnp.zeros_like(square)
@@ -478,7 +521,9 @@
             for d in range(2):
                 message(t - 1, d, H - 1).wait_recv()
                 total = total + rbuf[lax.rem(t - 1, 4), d, H - 1].astype(jnp.float32)
-            prod[pl.ds(pl.multiple_of(k * m, m), m), :] = total
+            at = pl.ds(pl.multiple_of(k * m, m), m)
+            prod[at, :] = total
+            pltpu.make_async_copy(prod.at[at], right_out.at[at], out_sem.at[2]).start()
             square[...] += jnp.sum(total * total, axis=0, keepdims=True)
 
         for h in range(H - 1, -1, -1):
@@ -508,8 +553,9 @@
                             sbuf[slot, d, h] = (fresh_part + came).astype(jnp.bfloat16)
                     message(t, d, h).start()
 
-        for at, work in ((6, left_sum), (8, left_product), (10, left_finish)):
-            pl.when(t == min(at, steps - 1))(work)
+        work = [(6, left_sum), (8, left_product), (10, left_finish)]
+        for at, run in work:
+            pl.when(t == min(at, steps - 1))(run)
 
     gather_sq[col] = jnp.broadcast_to(square[...], gather_sq.shape[1:])
     for j in range(1, C):
@@ -523,6 +569,8 @@
         half_copy(j, col).wait_send()
     for j in range(1, R):
         lsq_copy(j, row).wait_send()
+    for d in range(2):
+        basis_ring(d).wait_send()
     new_out.wait()
     prod_out.wait()
     for j in range(1, C):
@@ -530,26 +578,18 @@
     total = gather_sq[0]
     for c in range(1, C):
         total = total + gather_sq[c]
-    scale = lax.rsqrt(total[0:1] / dhidden + epsilon)
-
-    def put(k):
-        at = pl.ds(pl.multiple_of(k * m, m), m)
-        return pltpu.make_async_copy(prod.at[at], right_out.at[at], out_sem.at[2])
-
-    @pl.loop(0, count)
-    def _(k):
-        at = pl.ds(pl.multiple_of(k * m, m), m)
-        prod[at, :] = prod[at, :] * scale
-        put(k).start()
-
+    sum_sq[...] = total
+    put_sq = pltpu.make_async_copy(sum_sq, square_out, out_sem.at[3])
+    put_sq.start()
     for j in range(1, C):
         sq_copy(j, col).wait_send()
+    put_sq.wait()
     pltpu.make_async_copy(prod, right_out, out_sem.at[2]).wait()
 
 
-def product_stage(R, C, dhidden, fresh, vectors, left_part, basis, left_factor):
+def product_stage(R, C, dhidden, fresh, vectors, left_part, basis, came, left_factor):
     total_rows, depth = fresh.shape
-    m = 256
+    m = CHUNK
     H = R // 2
     width = vectors.shape[0] * vectors.shape[2] // R
     rows, lcols = left_factor.shape
@@ -560,11 +600,12 @@
         functools.partial(product_kernel, R, C, m, dhidden),
         out_shape=(
             jax.ShapeDtypeStruct((total_rows, width), f32),
+            jax.ShapeDtypeStruct((8, width), f32),
             jax.ShapeDtypeStruct((rows, lcols), f32),
             jax.ShapeDtypeStruct((rows, lcols), f32),
         ),
-        in_specs=[any_space] * 5,
-        out_specs=(any_space,) * 3,
+        in_specs=[any_space] * 7,
+        out_specs=(any_space,) * 4,
         scratch_shapes=[
             pltpu.VMEM(vectors.shape, bf16),
             pltpu.VMEM((2, m, depth), f32),
@@ -574,6 +615,7 @@
             pltpu.VMEM((total_rows, width), f32),
             pltpu.VMEM((1, width), f32),
             pltpu.VMEM((C, 8, width), f32),
+            pltpu.VMEM((8, width), f32),
             pltpu.VMEM((C, lcols, rows), f32),
             pltpu.VMEM((C, rows, lcols), bf16),
             pltpu.VMEM(basis.shape, bf16),
@@ -581,21 +623,59 @@
             pltpu.VMEM((rows, lcols), f32),
             pltpu.VMEM((rows, lcols), f32),
             pltpu.VMEM((R, 8, lcols), f32),
-            dma((4,)), dma((2,)), dma((2, 2, H)), dma((4, 2, H)), dma((C,)), dma((C,)),
-            dma((C,)), dma((C,)), dma((C,)), dma((C,)), dma((R,)), dma((R,)), dma((3,)),
+            dma((6,)), dma((2,)), dma((2, 2, H)), dma((4, 2, H)), dma((C,)), dma((C,)),
+            dma((C,)), dma((C,)), dma((C,)), dma((C,)), dma((R,)), dma((R,)), dma((2,)), dma((2,)), dma((4,)),
         ],
         compiler_params=pltpu.CompilerParams(
             collective_id=1, has_side_effects=True, vmem_limit_bytes=62 * 1024 * 1024),
         name="product_reduce",
-    )(fresh, vectors, left_part, basis, left_factor)
+    )(fresh, vectors, left_part, basis, *came, left_factor)
+
+
+def finish_kernel(dhidden, prod, square, left_new, left_prod, right_out, left_new_out, left_out):
+    right_out[...] = prod[...] * lax.rsqrt(square[0:1] / dhidden + epsilon)
+    left_new_out[...] = left_new[...]
+    left_out[...] = left_prod[...]
+
+
+def finish_stage(dhidden, prod, square, left_new, left_prod):
+    steps = 4
+    blocks = [
+        pl.BlockSpec((a.shape[0] // steps, a.shape[1]), lambda i: (i, 0))
+        for a in (prod, left_new, left_prod)
+    ]
+    return pl.pallas_call(
+        functools.partial(finish_kernel, dhidden),
+        grid=(steps,),
+        out_shape=tuple(jax.ShapeDtypeStruct(a.shape, a.dtype) for a in (prod, left_new, left_prod)),
+        in_specs=[blocks[0], pl.BlockSpec(square.shape, lambda i: (0, 0)), blocks[1], blocks[2]],
+        out_specs=tuple(blocks),
+        name="finish",
+    )(prod, square, left_new, left_prod)
 
 
 def make_body(R, C, dhidden):
+    members = [2 * p if p < R // 2 else 2 * (R - 1 - p) + 1 for p in range(R)]
+    forward = [(members[p], members[(p + 1) % R]) for p in range(R)]
+    backward = [(b, a) for a, b in forward]
+
     def on_device(gradient, left_factor, right_factor, left_basis, right_basis):
-        right_new, gram_part, left_basis_cols, vectors, _ = gather_stage(
+        row = lax.axis_index("row")
+        here = place_of(row, R)
+        partial, gram_part, left_basis_cols, vectors, last, match, _ = gather_stage(
             R, C, gradient, left_basis, right_basis, right_factor)
-        right_out, left_new, left_out = product_stage(
-            R, C, dhidden, right_new, vectors, gram_part, left_basis_cols, left_factor)
+        rows = left_basis.shape[0]
+        held = R // 2 - 2
+        came = []
+        for perm, away in ((forward, R - held), (backward, held)):
+            start = member_at(lax.rem(here + away, R), R) * rows
+            piece = lax.dynamic_slice_in_dim(left_basis_cols, start, rows, 0)
+            came.append(lax.ppermute(piece, "row", perm))
+        last, match = (a.reshape(-1, a.shape[-1]) for a in (last, match))
+        right_new = partial + (1.0 - ema_decay) * dot(last, match, ((0,), (0,)))
+        right_prod, square, left_new, left_out = product_stage(
+            R, C, dhidden, right_new, vectors, gram_part, left_basis_cols, came, left_factor)
+        right_out, left_new, left_out = finish_stage(dhidden, right_prod, square, left_new, left_out)
         return (left_new, right_new, left_out, right_out)
 
     return on_device

time: 454 us -> 439 us (0.967)
  local copies, waits for them, and re-layouts: 24 us -> 2.31 us
  matrix products: 0 us -> 18.1 us
  Pallas kernels: 429 us -> 416 us
    pallas_call x1, Pallas kernels: 271 us -> 248 us  [gather_stage(): pl.pallas_call(functools.partial(gather_kernel, R, C, tile), out_shape=(j...]
    unnamed x8 -> x4, local copies, waits for them, and re-layouts: 24 us -> 0.99 us
    dot_general x0 -> x1, matrix products: none -> 18.1 us  [dot(): lax.dot_general(a, b, (dims, ((), ())), preferred_element_type=jnp.float32)]
    pallas_call x0 -> x1, Pallas kernels: none -> 5.69 us  [finish_stage(): pl.pallas_call(functools.partial(finish_kernel, dhidden), grid=(steps,),...]
  transfers between devices with their start and end apart: 0 -> 2, of which waited for: 0 -> 0; matrix products, arithmetic and copies ran while one was open for 0% -> 4% of each run, Pallas kernels for 0% -> 0%
where the time goes in v1:
time: 439 us
  Pallas kernels  416 us (95%)
  matrix products  18.1 us (4%)
    pallas_call x1, Pallas kernels, gather_stage(): pl.pallas_call(functools.partial(gather_kernel, R, C, tile), out_shape=(j...  248 us
    pallas_call x1, Pallas kernels, product_stage(): pl.pallas_call(functools.partial(product_kernel, R, C, m, dhidden), out_s...  162 us
    dot_general x1, matrix products, dot(): lax.dot_general(a, b, (dims, ((), ())), preferred_element_type=jnp.float32)  18.1 us
  transfers between devices with their start and end apart: 2, of which 0 were waited for; matrix products, arithmetic and copies ran while one was open for 4% of the time, Pallas kernels for 0%

profile of v1, /device:TPU:0, one launch (start us, length us, event | category | flops | bytes accessed | tf_op | source)
XLA Modules:
  0.0 438.7 jit_solution(10579331758305824275)
XLA Ops:
  0.7 248.1 %gather_gram.1 = (f32[3584,1792]{1,0:T(8,128)}, f32[3072,384]{1,0:T(8,128)}, bf16[3072,768]{1,0:T(8,128)(2,1)}, bf16[4,1792,512]{2,1,0:T(8,128)(2,1)}, bf16[2,2,...) custom-call(bf16[384,3584]{1,0:T(8,128)(2,1)} %grad.1, ...), custom_call_target="tpu_custom_call" | custom-call | tf_op jit(solution)/shard_map/gather_gram/pallas_call | solution.py:307
  248.7 1.3 constant_dynamic-slice_fusion
  250.1 0.1 collective-permute-start
  250.1 2.0 collective-permute-start.1
  252.2 18.1 %fusion.fresh = f32[3584,1792]{1,0:T(8,128)} fusion(f32[3584,1792]{1,0:T(8,128)} %get-tuple-element.17, bf16[2,2,96,3584]{3,2,1,0:T(8,128)(2,1)} %get-tuple-element.18, bf16[2,2,96,1792]{3,2,1,0:T(8,128)(2,1)} %get-tuple-element.19), kind=kOutput, calls=%fused_computation.1 | convolution fusion | flops 4945346560 | bytes 55508992 | tf_op jit(solution)/shard_map/dot_general | solution.py:19
  270.2 0.0 collective-permute-done.came_forward
  270.2 0.0 copy-start
  270.2 0.0 collective-permute-done.1.came_back
  270.2 0.0 copy-start.1
  270.3 0.8 copy-done
  271.0 0.2 copy-done.1
  271.2 161.8 %product_reduce.1 = (f32[3584,256]{1,0:T(8,128)}, f32[8,256]{1,0:T(8,128)}, f32[384,768]{1,0:T(8,128)}, f32[384,768]{1,0:T(8,128)}) custom-call(f32[3584,1792]{1,0:T(8,128)} %fusion.fresh, bf16[4,1792,512]{2,1,0:T(8,128)(2,1)} %get-tuple-element.20.vectors, f32[3072,384]{1,0:T(8,128)} %get-tuple-element.21.left_part, ...), custom_call_target="tpu_custom_call" | custom-call | tf_op jit(solution)/shard_map/product_reduce/pallas_call | solution.py:599
  433.0 5.7 %finish.1 = (f32[3584,256]{1,0:T(8,128)}, f32[384,768]{1,0:T(8,128)}, f32[384,768]{1,0:T(8,128)}) custom-call(f32[3584,256]{1,0:T(8,128)} %get-tuple-element.23.prod, f32[8,256]{1,0:T(8,128)} %get-tuple-element.24.square, f32[384,768]{1,0:T(8,128)} %get-tuple-element.25.left_new, f32[384,768]{1,0:T(8,128)} %get-tuple-element.26.left_prod), custom_call_target="tpu_custom_call" | custom-call | tf_op jit(solution)/shard_map/finish/pallas_call | solution.py:647
Async XLA Ops:
  250.1 20.1 %collective-permute-start = (bf16[384,768]{1,0:T(8,128)(2,1)S(1)}, bf16[384,768]{1,0:T(8,128)(2,1)S(1)}, u32[]{:S(2)}, u32[]{:S(2)}) collective-permute-start(bf16[384,768]{1,0:T(8,128)(2,1)S(1)} %get-tuple-element.31), channel_id=1, source_target_pairs={{0,8},{8,16},{16,24},{24,28},{28,20},{20,12},{12,4},{4,0},{1,9},{9... | collective-permute-start | bytes 1769480 | tf_op jit(solution)/shard_map/ppermute | solution.py:673
  250.1 20.1 %collective-permute-start.1 = (bf16[384,768]{1,0:T(8,128)(2,1)S(1)}, bf16[384,768]{1,0:T(8,128)(2,1)S(1)}, u32[]{:S(2)}, u32[]{:S(2)}) collective-permute-start(bf16[384,768]{1,0:T(8,128)(2,1)S(1)} %get-tuple-element.30), channel_id=1, source_target_pairs={{8,0},{16,8},{24,16},{28,24},{20,28},{12,20},{4,12},{0,4},{9,1},{1... | collective-permute-start | bytes 1769480 | tf_op jit(solution)/shard_map/ppermute | solution.py:673
  270.2 0.8 copy-start
  270.2 1.0 copy-start.1

commit v2 on v1

--- a/solution.py
+++ b/solution.py
@@ -230,7 +230,7 @@
 
     relay_due = [(0, s) for s in range(SPLIT)]
     hops = R // 2 - 2
-    begin = R - hops
+    begin = R - 1 - hops
     for t in range(1, R):
         for s in range(SPLIT):
             for d in range(2):
@@ -239,7 +239,7 @@
                 for d in range(2):
                     ring(t, d, s).start()
             offer(t, s)
-            if s == SPLIT - 1 and t >= begin:
+            if s == SPLIT - 1 and begin <= t < last:
                 basis_hop(t - begin)
             for due in relay_due:
                 relay(*due)

time: 439 us -> 437 us (level)
  Pallas kernels: 416 us -> 410 us
    pallas_call x1, Pallas kernels: 248 us -> 241 us  [gather_stage(): pl.pallas_call(functools.partial(gather_kernel, R, C, tile), out_shape=(j...]
where the time goes in v2:
time: 437 us
  Pallas kernels  410 us (94%)
  matrix products  18.1 us (4%)
  starting transfers between devices  5.96 us (1%)
    pallas_call x1, Pallas kernels, gather_stage(): pl.pallas_call(functools.partial(gather_kernel, R, C, tile), out_shape=(j...  241 us
    pallas_call x1, Pallas kernels, product_stage(): pl.pallas_call(functools.partial(product_kernel, R, C, m, dhidden), out_s...  164 us
    dot_general x1, matrix products, dot(): lax.dot_general(a, b, (dims, ((), ())), preferred_element_type=jnp.float32)  18.1 us
  transfers between devices with their start and end apart: 2, of which 0 were waited for; matrix products, arithmetic and copies ran while one was open for 4% of the time, Pallas kernels for 0%

profile of v2, /device:TPU:0, one launch (start us, length us, event | category | flops | bytes accessed | tf_op | source)
XLA Modules:
  0.0 436.9 jit_solution(9465988242558319742)
XLA Ops:
  0.7 240.5 %gather_gram.1 = (f32[3584,1792]{1,0:T(8,128)}, f32[3072,384]{1,0:T(8,128)}, bf16[3072,768]{1,0:T(8,128)(2,1)}, bf16[4,1792,512]{2,1,0:T(8,128)(2,1)}, bf16[2,2,...) custom-call(bf16[384,3584]{1,0:T(8,128)(2,1)} %grad.1, ...), custom_call_target="tpu_custom_call" | custom-call | tf_op jit(solution)/shard_map/gather_gram/pallas_call | solution.py:307
  241.2 1.3 constant_dynamic-slice_fusion
  242.5 6.0 %collective-permute-start = (bf16[384,768]{1,0:T(8,128)(2,1)S(1)}, bf16[384,768]{1,0:T(8,128)(2,1)S(1)}, u32[]{:S(2)}, u32[]{:S(2)}) collective-permute-start(bf16[384,768]{1,0:T(8,128)(2,1)S(1)} %get-tuple-element.31), channel_id=1, source_target_pairs={{0,8},{8,16},{16,24},{24,28},{28,20},{20,12},{12,4},{4,0},{1,9},{9... | collective-permute-start | bytes 1769480 | tf_op jit(solution)/shard_map/ppermute | solution.py:673
  248.5 0.0 collective-permute-start.1
  248.5 18.1 %fusion.fresh = f32[3584,1792]{1,0:T(8,128)} fusion(f32[3584,1792]{1,0:T(8,128)} %get-tuple-element.17, bf16[2,2,96,3584]{3,2,1,0:T(8,128)(2,1)} %get-tuple-element.18, bf16[2,2,96,1792]{3,2,1,0:T(8,128)(2,1)} %get-tuple-element.19), kind=kOutput, calls=%fused_computation.1 | convolution fusion | flops 4945346560 | bytes 55508992 | tf_op jit(solution)/shard_map/dot_general | solution.py:19
  266.6 0.0 collective-permute-done.came_forward
  266.6 0.0 copy-start
  266.6 0.0 collective-permute-done.1.came_back
  266.6 0.0 copy-start.1
  266.6 0.8 copy-done
  267.4 0.2 copy-done.1
  267.6 163.7 %product_reduce.1 = (f32[3584,256]{1,0:T(8,128)}, f32[8,256]{1,0:T(8,128)}, f32[384,768]{1,0:T(8,128)}, f32[384,768]{1,0:T(8,128)}) custom-call(f32[3584,1792]{1,0:T(8,128)} %fusion.fresh, bf16[4,1792,512]{2,1,0:T(8,128)(2,1)} %get-tuple-element.20.vectors, f32[3072,384]{1,0:T(8,128)} %get-tuple-element.21.left_part, ...), custom_call_target="tpu_custom_call" | custom-call | tf_op jit(solution)/shard_map/product_reduce/pallas_call | solution.py:599
  431.2 5.7 %finish.1 = (f32[3584,256]{1,0:T(8,128)}, f32[384,768]{1,0:T(8,128)}, f32[384,768]{1,0:T(8,128)}) custom-call(f32[3584,256]{1,0:T(8,128)} %get-tuple-element.23.prod, f32[8,256]{1,0:T(8,128)} %get-tuple-element.24.square, f32[384,768]{1,0:T(8,128)} %get-tuple-element.25.left_new, f32[384,768]{1,0:T(8,128)} %get-tuple-element.26.left_prod), custom_call_target="tpu_custom_call" | custom-call | tf_op jit(solution)/shard_map/finish/pallas_call | solution.py:647
Async XLA Ops:
  242.5 24.0 %collective-permute-start = (bf16[384,768]{1,0:T(8,128)(2,1)S(1)}, bf16[384,768]{1,0:T(8,128)(2,1)S(1)}, u32[]{:S(2)}, u32[]{:S(2)}) collective-permute-start(bf16[384,768]{1,0:T(8,128)(2,1)S(1)} %get-tuple-element.31), channel_id=1, source_target_pairs={{0,8},{8,16},{16,24},{24,28},{28,20},{20,12},{12,4},{4,0},{1,9},{9... | collective-permute-start | bytes 1769480 | tf_op jit(solution)/shard_map/ppermute | solution.py:673
  248.5 18.1 %collective-permute-start.1 = (bf16[384,768]{1,0:T(8,128)(2,1)S(1)}, bf16[384,768]{1,0:T(8,128)(2,1)S(1)}, u32[]{:S(2)}, u32[]{:S(2)}) collective-permute-start(bf16[384,768]{1,0:T(8,128)(2,1)S(1)} %get-tuple-element.30), channel_id=1, source_target_pairs={{8,0},{16,8},{24,16},{28,24},{20,28},{12,20},{4,12},{0,4},{9,1},{1... | collective-permute-start | bytes 1769480 | tf_op jit(solution)/shard_map/ppermute | solution.py:673
  266.6 0.8 copy-start
  266.6 1.0 copy-start.1
